TPU v7x, 256 devices: a whole 4x4x8 slice. The times are simulated.
256 devices in a mesh: row: 16 (over x, y), col: 16 (over z, core).
Axes of the slice: x: 4, y: 4, z: 8, core: 2. Of those that a mesh axis runs over, the one named last changes fastest.
Arguments:
- values: bfloat16 [8192, 8192], P('row', 'col'), may hold values from 0.0001296997 to 0.12988281
- tile_mask: int32 [64, 64], P('row', 'col'), may hold values 0 or 1
- keep_mask: int32 [64, 64], P('row', 'col'), may hold values 0 or 1
- thr_index: int32 [8192], P('col'), may hold values from 0 to 9
Outputs:
- expanded: bfloat16 [8192, 8192], P('row', 'col')
All inputs are finite; a program needn't handle non-finite values. No bound on the sum of `tile_mask` or of `keep_mask` on one device may be relied on, other than what follows from the above.
Results may differ from a plain program's by a relative error of at most 0.0004.
Values may be sent and summed in bfloat16 or wider, within the bound.
A program may use at most 64 MiB of HBM per device.

v0:
```python
import jax
import jax.numpy as jnp
from jax import lax
from jax.sharding import Mesh
from jax.sharding import PartitionSpec as P

TB = 128
ROW = ("row_0", "row_1")


def over_axes(x, axes):
    for axis in axes:
        x = lax.psum(x, axis)
    return x


def on_device(values, tile_mask, keep_mask, thr_index):
    row_count, col_count = values.shape
    row_tiles = row_count // TB
    col_tiles = col_count // TB
    matrix = (
        values.reshape(row_tiles, TB, col_tiles, TB)
        * tile_mask[:, None, :, None].astype(jnp.bfloat16)
    ).reshape(row_count, col_count)
    kept_cells = jnp.broadcast_to(
        keep_mask[:, None, :, None].astype(jnp.float32), (row_tiles, TB, col_tiles, TB)
    ).reshape(row_count, col_count)
    order_all = row_count * lax.axis_size(ROW)
    thresholds = 0.125 * thr_index.astype(jnp.float32)
    col_panel = lax.all_gather(matrix, ROW, axis=0, tiled=True)
    product = jnp.dot(
        lax.all_gather(matrix, "col", axis=1, tiled=True),
        col_panel,
        preferred_element_type=jnp.float32,
    )
    outputs = []
    for phase_idx in range(col_tiles):
        lo_col = phase_idx * TB
        part_prod = product[:, lo_col : lo_col + TB]
        col_means = over_axes(jnp.sum(part_prod, axis=0), ROW) / order_all
        pruned = (
            jnp.maximum(part_prod - thresholds[lo_col : lo_col + TB] * col_means, 0.0)
            * kept_cells[:, lo_col : lo_col + TB]
        )
        col_totals = over_axes(jnp.sum(pruned, axis=0), ROW) / order_all
        outputs.append(pruned / jnp.maximum(col_totals, 0.1))
    result = jnp.concatenate(outputs, axis=1)
    return result.astype(jnp.bfloat16)


def solution(mesh):
    finer = Mesh(mesh.devices.reshape(4, 4, mesh.shape["col"]), ("row_0", "row_1", "col"))
    placed = (P(ROW, "col"), P(ROW, "col"), P(ROW, "col"), P("col"))
    return jax.shard_map(
        on_device, mesh=finer, in_specs=placed, out_specs=P(ROW, "col"), check_vma=False
    )
```

profile of v0, /device:TPU:2, one launch (start us, length us, event | category | flops | bytes accessed | tf_op | source)
XLA Modules:
  0.0 198.9 jit_solution(1561034129201004434)
XLA Ops:
  6.5 0.0 all-gather.3.cloned.1.call-start
  6.5 0.7 convert_element_type.12
  7.2 0.2 mul.41
  7.4 1.9 bitcast_multiply_fusion
  9.3 0.0 all-gather.3.cloned.1.call-update
  9.4 0.0 all-gather.5.cloned.1.call-start
  9.4 0.7 all-gather.5.cloned.1.call-update
  10.1 0.7 convert_element_type.14
  10.8 0.2 broadcast_in_dim.2
  11.0 0.1 copy.9
  11.1 0.7 convert_multiply_fusion
  11.8 56.5 %all-gather.3.cloned.1.call-done = bf16[512,8192]{1,0:T(8,128)(2,1)} async-done(((bf16[512,512]{1,0:T(8,128)(2,1)}), bf16[512,8192]{1,0:T(8,128)(2,1)}) %all-gather.3.cloned.1.call-update) | async-done | bytes 8388624 | tf_op jit(solution)/shard_map/all_gather | solution.py:32
  68.3 76.8 %all-gather.5.cloned.1.call-done = bf16[8192,512]{1,0:T(8,128)(2,1)} async-done(((bf16[512,512]{1,0:T(8,128)(2,1)}), bf16[8192,512]{1,0:T(8,128)(2,1)}) %all-gather.5.cloned.1.call-update) | async-done | bytes 8388624 | tf_op jit(solution)/shard_map/all_gather | solution.py:30
  145.1 9.4 %fusion.4 = f32[512,512]{1,0:T(8,128)S(1)} fusion(bf16[512,8192]{1,0:T(8,128)(2,1)} %all-gather.3.cloned.1.call-done, bf16[8192,512]{1,0:T(8,128)(2,1)} %all-gather.5.cloned.1.call-done), kind=kOutput, calls=%fused_computation.28 | convolution fusion | flops 4294967296 | bytes 17825792 | tf_op jit(solution)/shard_map/dot_general | solution.py:31
  154.6 0.1 slice_reduce_fusion.3
  154.7 8.6 %all-reduce.3 = (f32[128]{0:T(128)S(1)}, f32[128]{0:T(128)S(1)}, f32[128]{0:T(128)S(1)}, f32[128]{0:T(128)S(1)}) all-reduce(f32[128]{0:T(128)S(1)} %get-tuple-element.9, f32[128]{0:T(128)S(1)} %get-tuple-element.10, f32[128]{0:T(128)S(1)} %get-tuple-element.11, ...), channel_id=1, replica_groups=mesh['row_0'=4,'row_1'=4,'col'=16] {'row_0'}, use_global_device_ids=true, to_apply=%region_1.0 | all-reduce | flops 512 | bytes 4096 | tf_op jit(solution)/shard_map/psum | solution.py:13
  163.3 10.1 %all-reduce.1 = (f32[128]{0:T(128)S(1)}, f32[128]{0:T(128)S(1)}, f32[128]{0:T(128)S(1)}, f32[128]{0:T(128)S(1)}) all-reduce(f32[128]{0:T(128)S(1)} %get-tuple-element.25, f32[128]{0:T(128)S(1)} %get-tuple-element.26, f32[128]{0:T(128)S(1)} %get-tuple-element.27, ...), channel_id=1, replica_groups=mesh['row_0'=4,'row_1'=4,'col'=16] {'row_1'}, use_global_device_ids=true, to_apply=%region_2.0 | all-reduce | flops 512 | bytes 4096 | tf_op jit(solution)/shard_map/psum | solution.py:13
  173.4 0.2 fusion
  173.5 8.6 %all-reduce.2 = (f32[128]{0:T(128)S(1)}, f32[128]{0:T(128)S(1)}, f32[128]{0:T(128)S(1)}, f32[128]{0:T(128)S(1)}) all-reduce(f32[128]{0:T(128)S(1)} %get-tuple-element.6, f32[128]{0:T(128)S(1)} %get-tuple-element.7, f32[128]{0:T(128)S(1)} %get-tuple-element.8, ...), channel_id=1, replica_groups=mesh['row_0'=4,'row_1'=4,'col'=16] {'row_0'}, use_global_device_ids=true, to_apply=%region_22.0 | all-reduce | flops 512 | bytes 4096 | tf_op jit(solution)/shard_map/psum | solution.py:13
  182.1 8.9 %all-reduce = (f32[128]{0:T(128)S(1)}, f32[128]{0:T(128)S(1)}, f32[128]{0:T(128)S(1)}, f32[128]{0:T(128)S(1)}) all-reduce(f32[128]{0:T(128)S(1)} %get-tuple-element.21, f32[128]{0:T(128)S(1)} %get-tuple-element.22, f32[128]{0:T(128)S(1)} %get-tuple-element.23, ...), channel_id=1, replica_groups=mesh['row_0'=4,'row_1'=4,'col'=16] {'row_1'}, use_global_device_ids=true, to_apply=%region_23.0 | all-reduce | flops 512 | bytes 4096 | tf_op jit(solution)/shard_map/psum | solution.py:13
  191.1 0.2 divide_convert_fusion.3
  191.2 0.9 pad_maximum_fusion
  (3 shorter events, 0.0 us)
Async XLA Ops:
  6.5 61.8 %all-gather.3.cloned.1.call-start = ((), (), s32[]{:S(2)}) async-start(), calls=%async_computation | async-start | bytes 8912896 | tf_op jit(solution)/shard_map/all_gather | solution.py:32
  9.4 135.8 %all-gather.5.cloned.1.call-start = ((), (), s32[]{:S(2)}) async-start(), calls=%async_computation.1 | async-start | bytes 8912896 | tf_op jit(solution)/shard_map/all_gather | solution.py:30
Sparse Core Ops, SparseCore 0:
  9.5 58.7 all-gather.2
  70.7 74.3 all-gather.4
where the time goes:
time: 199 us
  waiting for transfers between devices  134 us (67%)
  blocking collectives  36.2 us (18%)
  between operations  13.4 us (7%)
  matrix products  9.44 us (5%)
  other arithmetic  5.27 us (3%)
    all_gather x1, waiting for transfers between devices, on_device(): col_panel = lax.all_gather(matrix, ROW, axis=0, tiled=True)  76.8 us
    all_gather x1, waiting for transfers between devices, on_device(): lax.all_gather(matrix, 'col', axis=1, tiled=True)  56.5 us
    psum x4, blocking collectives, over_axes(): x = lax.psum(x, axis)  36.2 us
    dot_general x1, matrix products, on_device(): jnp.dot(lax.all_gather(matrix, 'col', axis=1, tiled=True), col_panel, pre...  9.44 us
  transfers between devices with their start and end apart: 2, of which 2 were waited for; matrix products, arithmetic and copies ran while one was open for 1% of the time, Pallas kernels for 0%

commit v1 on v0

--- a/solution.py
+++ b/solution.py
@@ -29,7 +29,9 @@
     thresholds = 0.125 * thr_index.astype(jnp.float32)
     col_panel = lax.all_gather(matrix, ROW, axis=0, tiled=True)
     product = jnp.dot(
-        lax.all_gather(matrix, "col", axis=1, tiled=True),
+        jnp.concatenate(
+            lax.all_to_all(jnp.stack([matrix] * lax.axis_size("col")), "col", 0, 0), axis=1
+        ),
         col_panel,
         preferred_element_type=jnp.float32,
     )

time: 199 us -> 261 us (1.31)
  waiting for transfers between devices: 134 us -> 184 us
  starting transfers between devices: 0.04 us -> 8.79 us
  local copies, waits for them, and re-layouts: 0.48 us -> 4.74 us
    all_to_all x0 -> x1, waiting for transfers between devices: none -> 183 us  [on_device(): lax.all_to_all(jnp.stack([matrix] * lax.axis_size('col')), 'col', 0, 0)]
    all_gather x1, waiting for transfers between devices: 76.8 us -> 0.01 us  [on_device(): col_panel = lax.all_gather(matrix, ROW, axis=0, tiled=True)]
    all_gather x1 -> x0, waiting for transfers between devices: 56.5 us -> none  [on_device(): lax.all_gather(matrix, 'col', axis=1, tiled=True)]
    all_to_all x0 -> x1, starting transfers between devices: none -> 8.75 us  [on_device(): lax.all_to_all(jnp.stack([matrix] * lax.axis_size('col')), 'col', 0, 0)]
    another operation x0 -> x1, local copies, waits for them, and re-layouts: none -> 4.03 us  [on_device(): jnp.stack([matrix] * lax.axis_size('col'))]
  transfers between devices with their start and end apart: 2 -> 2, of which waited for: 2 -> 1; matrix products, arithmetic and copies ran while one was open for 1% -> 0% of each run, Pallas kernels for 0% -> 0%
where the time goes in v1:
time: 261 us
  waiting for transfers between devices  184 us (70%)
  blocking collectives  37.2 us (14%)
  between operations  13.5 us (5%)
  matrix products  9.5 us (4%)
  starting transfers between devices  8.79 us (3%)
  local copies, waits for them, and re-layouts  4.74 us (2%)
  other arithmetic  3.11 us (1%)
    all_to_all x1, waiting for transfers between devices, on_device(): lax.all_to_all(jnp.stack([matrix] * lax.axis_size('col')), 'col', 0, 0)  183 us
    psum x4, blocking collectives, over_axes(): x = lax.psum(x, axis)  37.2 us
    dot_general x1, matrix products, on_device(): jnp.dot(jnp.concatenate(lax.all_to_all(jnp.stack([matrix] * lax.axis_size...  9.5 us
    all_to_all x1, starting transfers between devices, on_device(): lax.all_to_all(jnp.stack([matrix] * lax.axis_size('col')), 'col', 0, 0)  8.75 us
  transfers between devices with their start and end apart: 2, of which 1 were waited for; matrix products, arithmetic and copies ran while one was open for 0% of the time, Pallas kernels for 0%

profile of v1, /device:TPU:2, one launch (start us, length us, event | category | flops | bytes accessed | tf_op | source)
XLA Modules:
  0.0 260.7 jit_solution(11468512159247498030)
XLA Ops:
  6.5 0.7 convert_element_type.12
  7.2 0.2 mul.43
  7.4 1.1 bitcast_multiply_fusion
  8.5 0.0 copy-start
  8.6 0.2 copy.5
  8.8 4.0 %stack.3 = bf16[16,512,512]{1,2,0:T(8,128)(2,1)} broadcast(bf16[512,512]{0,1:T(8,128)(2,1)S(1)} %copy.5), dimensions={1,2} | broadcast | bytes 8912896 | tf_op jit(solution)/shard_map/stack | solution.py:33
  12.8 0.0 copy-start.1
  12.8 0.0 copy-start.2
  12.8 0.0 copy-done
  12.8 8.8 %all-to-all-start = ((bf16[16,512,512]{1,2,0:T(8,128)(2,1)}), bf16[16,512,512]{1,2,0:T(8,128)(2,1)}, u32[]{:S(2)}, u32[]{:S(2)}) async-start(bf16[16,512,512]{1,2,0:T(8,128)(2,1)} %stack.3), calls=%async_computation | async-start | bytes 16777216 | tf_op jit(solution)/shard_map/all_to_all | solution.py:33
  21.6 0.0 all-gather.2.cloned.1.call-start
  21.6 0.7 all-gather.2.cloned.1.call-update
  22.3 0.0 copy-done.1
  22.3 0.2 broadcast_in_dim.2
  22.5 0.1 copy.10
  22.6 0.0 copy-done.2
  22.6 183.1 %all-to-all-done = bf16[16,512,512]{1,2,0:T(8,128)(2,1)} async-done(((bf16[16,512,512]{1,2,0:T(8,128)(2,1)}), bf16[16,512,512]{1,2,0:T(8,128)(2,1)}, u32[]{:S(2)}, u32[]{:S(2)}) %all-to-all-start) | async-done | bytes 8388640 | tf_op jit(solution)/shard_map/all_to_all | solution.py:33
  205.8 0.0 all-gather.2.cloned.1.call-done
  205.8 9.5 %fusion.4 = f32[512,512]{1,0:T(8,128)S(1)} fusion(bf16[512,8192]{0,1:T(8,128)(2,1)} %bitcast.1, bf16[8192,512]{1,0:T(8,128)(2,1)} %all-gather.2.cloned.1.call-done), kind=kOutput, calls=%fused_computation.28 | convolution fusion | flops 4294967296 | bytes 17825792 | tf_op jit(solution)/shard_map/dot_general | solution.py:31
  215.3 0.1 slice_reduce_fusion.3
  215.4 8.6 %all-reduce.3 = (f32[128]{0:T(128)S(1)}, f32[128]{0:T(128)S(1)}, f32[128]{0:T(128)S(1)}, f32[128]{0:T(128)S(1)}) all-reduce(f32[128]{0:T(128)S(1)} %get-tuple-element.9, f32[128]{0:T(128)S(1)} %get-tuple-element.10, f32[128]{0:T(128)S(1)} %get-tuple-element.11, ...), channel_id=1, replica_groups=mesh['row_0'=4,'row_1'=4,'col'=16] {'row_0'}, use_global_device_ids=true, to_apply=%region_1.0 | all-reduce | flops 512 | bytes 4096 | tf_op jit(solution)/shard_map/psum | solution.py:13
  224.0 10.7 %all-reduce.1 = (f32[128]{0:T(128)S(1)}, f32[128]{0:T(128)S(1)}, f32[128]{0:T(128)S(1)}, f32[128]{0:T(128)S(1)}) all-reduce(f32[128]{0:T(128)S(1)} %get-tuple-element.25, f32[128]{0:T(128)S(1)} %get-tuple-element.26, f32[128]{0:T(128)S(1)} %get-tuple-element.27, ...), channel_id=1, replica_groups=mesh['row_0'=4,'row_1'=4,'col'=16] {'row_1'}, use_global_device_ids=true, to_apply=%region_2.0 | all-reduce | flops 512 | bytes 4096 | tf_op jit(solution)/shard_map/psum | solution.py:13
  234.8 0.2 fusion
  234.9 10.1 %all-reduce.2 = (f32[128]{0:T(128)S(1)}, f32[128]{0:T(128)S(1)}, f32[128]{0:T(128)S(1)}, f32[128]{0:T(128)S(1)}) all-reduce(f32[128]{0:T(128)S(1)} %get-tuple-element.6, f32[128]{0:T(128)S(1)} %get-tuple-element.7, f32[128]{0:T(128)S(1)} %get-tuple-element.8, ...), channel_id=1, replica_groups=mesh['row_0'=4,'row_1'=4,'col'=16] {'row_0'}, use_global_device_ids=true, to_apply=%region_22.0 | all-reduce | flops 512 | bytes 4096 | tf_op jit(solution)/shard_map/psum | solution.py:13
  245.1 7.7 %all-reduce = (f32[128]{0:T(128)S(1)}, f32[128]{0:T(128)S(1)}, f32[128]{0:T(128)S(1)}, f32[128]{0:T(128)S(1)}) all-reduce(f32[128]{0:T(128)S(1)} %get-tuple-element.21, f32[128]{0:T(128)S(1)} %get-tuple-element.22, f32[128]{0:T(128)S(1)} %get-tuple-element.23, ...), channel_id=1, replica_groups=mesh['row_0'=4,'row_1'=4,'col'=16] {'row_1'}, use_global_device_ids=true, to_apply=%region_23.0 | all-reduce | flops 512 | bytes 4096 | tf_op jit(solution)/shard_map/psum | solution.py:13
  252.8 0.2 divide_convert_fusion.3
  253.0 0.9 pad_maximum_fusion
  (5 shorter events, 0.0 us)
Async XLA Ops:
  8.5 4.3 %copy-start = (bf16[512,512]{1,0:T(8,128)(2,1)}, bf16[512,512]{1,0:T(8,128)(2,1)S(1)}, u32[]{:S(2)}) copy-start(bf16[512,512]{1,0:T(8,128)(2,1)S(1)} %bitcast_multiply_fusion) | copy-start | bytes 1572868
  12.8 9.5 %copy-start.1 = (s32[4,4]{1,0:T(4,128)S(1)}, s32[4,4]{1,0:T(4,128)}, u32[]{:S(2)}) copy-start(s32[4,4]{1,0:T(4,128)} %param.6) | copy-start | bytes 196
  12.8 9.8 %copy-start.2 = (s32[512]{0:T(512)S(1)}, s32[512]{0:T(512)}, u32[]{:S(2)}) copy-start(s32[512]{0:T(512)} %param.7) | copy-start | bytes 6148
  12.8 193.0 %all-to-all-start = ((bf16[16,512,512]{1,2,0:T(8,128)(2,1)}), bf16[16,512,512]{1,2,0:T(8,128)(2,1)}, u32[]{:S(2)}, u32[]{:S(2)}) async-start(bf16[16,512,512]{1,2,0:T(8,128)(2,1)} %stack.3), calls=%async_computation | async-start | bytes 16777216 | tf_op jit(solution)/shard_map/all_to_all | solution.py:33
  21.6 184.2 %all-gather.2.cloned.1.call-start = ((), (), s32[]{:S(2)}) async-start(), calls=%async_computation.1 | async-start | bytes 8912896 | tf_op jit(solution)/shard_map/all_gather | solution.py:30
Sparse Core Ops, SparseCore 0:
  24.8 77.3 all-gather.1

commit v2 on v0

--- a/solution.py
+++ b/solution.py
@@ -10,7 +10,7 @@
 
 def over_axes(x, axes):
     for axis in axes:
-        x = lax.psum(x, axis)
+        x = jnp.sum(lax.all_gather(x, axis), axis=0)
     return x
 
 

time: 199 us -> 292 us (1.47)
  blocking collectives: 36.2 us -> 129 us
    all_gather x0 -> x16, blocking collectives: none -> 129 us  [over_axes(): x = jnp.sum(lax.all_gather(x, axis), axis=0)]
    psum x4 -> x0, blocking collectives: 36.2 us -> none  [over_axes(): x = lax.psum(x, axis)]
where the time goes in v2:
time: 292 us
  waiting for transfers between devices  134 us (46%)
  blocking collectives  129 us (44%)
  between operations  13.5 us (5%)
  matrix products  9.44 us (3%)
  other arithmetic  5.63 us (2%)
    all_gather x16, blocking collectives, over_axes(): x = jnp.sum(lax.all_gather(x, axis), axis=0)  129 us
    all_gather x1, waiting for transfers between devices, on_device(): col_panel = lax.all_gather(matrix, ROW, axis=0, tiled=True)  76.8 us
    all_gather x1, waiting for transfers between devices, on_device(): lax.all_gather(matrix, 'col', axis=1, tiled=True)  56.5 us
    dot_general x1, matrix products, on_device(): jnp.dot(lax.all_gather(matrix, 'col', axis=1, tiled=True), col_panel, pre...  9.44 us
  transfers between devices with their start and end apart: 2, of which 2 were waited for; matrix products, arithmetic and copies ran while one was open for 1% of the time, Pallas kernels for 0%

profile of v2, /device:TPU:2, one launch (start us, length us, event | category | flops | bytes accessed | tf_op | source)
XLA Modules:
  0.0 291.9 jit_solution(15835337287543353605)
XLA Ops:
  6.5 0.0 all-gather.35.cloned.1.call-start
  6.5 0.7 convert_element_type.12
  7.2 0.2 mul.41
  7.4 1.9 bitcast_multiply_fusion
  9.3 0.0 all-gather.35.cloned.1.call-update
  9.4 0.0 all-gather.37.cloned.1.call-start
  9.4 0.7 all-gather.37.cloned.1.call-update
  10.1 0.7 convert_element_type.14
  10.8 0.2 broadcast_in_dim.2
  11.0 0.1 copy.9
  11.1 0.7 convert_multiply_fusion
  11.8 56.5 %all-gather.35.cloned.1.call-done = bf16[512,8192]{1,0:T(8,128)(2,1)} async-done(((bf16[512,512]{1,0:T(8,128)(2,1)}), bf16[512,8192]{1,0:T(8,128)(2,1)}) %all-gather.35.cloned.1.call-update) | async-done | bytes 8388624 | tf_op jit(solution)/shard_map/all_gather | solution.py:32
  68.3 76.8 %all-gather.37.cloned.1.call-done = bf16[8192,512]{1,0:T(8,128)(2,1)} async-done(((bf16[512,512]{1,0:T(8,128)(2,1)}), bf16[8192,512]{1,0:T(8,128)(2,1)}) %all-gather.37.cloned.1.call-update) | async-done | bytes 8388624 | tf_op jit(solution)/shard_map/all_gather | solution.py:30
  145.1 9.4 %fusion.4 = f32[512,512]{1,0:T(8,128)S(1)} fusion(bf16[512,8192]{1,0:T(8,128)(2,1)} %all-gather.35.cloned.1.call-done, bf16[8192,512]{1,0:T(8,128)(2,1)} %all-gather.37.cloned.1.call-done), kind=kOutput, calls=%fused_computation.28 | convolution fusion | flops 4294967296 | bytes 17825792 | tf_op jit(solution)/shard_map/dot_general | solution.py:31
  154.6 0.1 slice_reduce_fusion.3
  154.7 7.8 %all-gather.16 = f32[4,1,128]{2,1,0:T(1,128)S(1)} all-gather(f32[1,1,128]{2,1,0:T(1,128)S(1)} %bitcast.34), channel_id=2, replica_groups=mesh['row_0'=4,'row_1'=4,'col'=16] {'row_0'}, dimensions={0}, use_global_device_ids=true | all-gather | bytes 2560 | tf_op jit(solution)/shard_map/all_gather | solution.py:13
  162.5 9.3 %all-gather.17 = f32[4,1,128]{2,1,0:T(1,128)S(1)} all-gather(f32[1,1,128]{2,1,0:T(1,128)S(1)} %bitcast.35), channel_id=3, replica_groups=mesh['row_0'=4,'row_1'=4,'col'=16] {'row_1'}, dimensions={0}, use_global_device_ids=true | all-gather | bytes 2560 | tf_op jit(solution)/shard_map/all_gather | solution.py:13
  171.9 7.8 %all-gather.20 = f32[4,1,128]{2,1,0:T(1,128)S(1)} all-gather(f32[1,1,128]{2,1,0:T(1,128)S(1)} %bitcast.33), channel_id=6, replica_groups=mesh['row_0'=4,'row_1'=4,'col'=16] {'row_0'}, dimensions={0}, use_global_device_ids=true | all-gather | bytes 2560 | tf_op jit(solution)/shard_map/all_gather | solution.py:13
  179.7 8.1 %all-gather.21 = f32[4,1,128]{2,1,0:T(1,128)S(1)} all-gather(f32[1,1,128]{2,1,0:T(1,128)S(1)} %bitcast.36), channel_id=7, replica_groups=mesh['row_0'=4,'row_1'=4,'col'=16] {'row_1'}, dimensions={0}, use_global_device_ids=true | all-gather | bytes 2560 | tf_op jit(solution)/shard_map/all_gather | solution.py:13
  187.9 7.0 %all-gather.24 = f32[4,1,128]{2,1,0:T(1,128)S(1)} all-gather(f32[1,1,128]{2,1,0:T(1,128)S(1)} %bitcast.32), channel_id=10, replica_groups=mesh['row_0'=4,'row_1'=4,'col'=16] {'row_0'}, dimensions={0}, use_global_device_ids=true | all-gather | bytes 2560 | tf_op jit(solution)/shard_map/all_gather | solution.py:13
  194.9 9.0 %all-gather.25 = f32[4,1,128]{2,1,0:T(1,128)S(1)} all-gather(f32[1,1,128]{2,1,0:T(1,128)S(1)} %bitcast.37), channel_id=11, replica_groups=mesh['row_0'=4,'row_1'=4,'col'=16] {'row_1'}, dimensions={0}, use_global_device_ids=true | all-gather | bytes 2560 | tf_op jit(solution)/shard_map/all_gather | solution.py:13
  203.9 7.8 %all-gather.28 = f32[4,1,128]{2,1,0:T(1,128)S(1)} all-gather(f32[1,1,128]{2,1,0:T(1,128)S(1)} %bitcast.31), channel_id=14, replica_groups=mesh['row_0'=4,'row_1'=4,'col'=16] {'row_0'}, dimensions={0}, use_global_device_ids=true | all-gather | bytes 2560 | tf_op jit(solution)/shard_map/all_gather | solution.py:13
  211.7 8.1 %all-gather.29 = f32[4,1,128]{2,1,0:T(1,128)S(1)} all-gather(f32[1,1,128]{2,1,0:T(1,128)S(1)} %bitcast.38), channel_id=15, replica_groups=mesh['row_0'=4,'row_1'=4,'col'=16] {'row_1'}, dimensions={0}, use_global_device_ids=true | all-gather | bytes 2560 | tf_op jit(solution)/shard_map/all_gather | solution.py:13
  219.9 0.2 fusion
  220.0 7.0 %all-gather.30 = f32[4,1,128]{2,1,0:T(1,128)S(1)} all-gather(f32[1,1,128]{2,1,0:T(1,128)S(1)} %bitcast.46), channel_id=16, replica_groups=mesh['row_0'=4,'row_1'=4,'col'=16] {'row_0'}, dimensions={0}, use_global_device_ids=true | all-gather | bytes 2560 | tf_op jit(solution)/shard_map/all_gather | solution.py:13
  227.1 9.0 %all-gather.31 = f32[4,1,128]{2,1,0:T(1,128)S(1)} all-gather(f32[1,1,128]{2,1,0:T(1,128)S(1)} %bitcast.39), channel_id=17, replica_groups=mesh['row_0'=4,'row_1'=4,'col'=16] {'row_1'}, dimensions={0}, use_global_device_ids=true | all-gather | bytes 2560 | tf_op jit(solution)/shard_map/all_gather | solution.py:13
  236.1 7.8 %all-gather.26 = f32[4,1,128]{2,1,0:T(1,128)S(1)} all-gather(f32[1,1,128]{2,1,0:T(1,128)S(1)} %bitcast.45), channel_id=12, replica_groups=mesh['row_0'=4,'row_1'=4,'col'=16] {'row_0'}, dimensions={0}, use_global_device_ids=true | all-gather | bytes 2560 | tf_op jit(solution)/shard_map/all_gather | solution.py:13
  243.9 8.1 %all-gather.27 = f32[4,1,128]{2,1,0:T(1,128)S(1)} all-gather(f32[1,1,128]{2,1,0:T(1,128)S(1)} %bitcast.40), channel_id=13, replica_groups=mesh['row_0'=4,'row_1'=4,'col'=16] {'row_1'}, dimensions={0}, use_global_device_ids=true | all-gather | bytes 2560 | tf_op jit(solution)/shard_map/all_gather | solution.py:13
  252.1 7.0 %all-gather.22 = f32[4,1,128]{2,1,0:T(1,128)S(1)} all-gather(f32[1,1,128]{2,1,0:T(1,128)S(1)} %bitcast.44), channel_id=8, replica_groups=mesh['row_0'=4,'row_1'=4,'col'=16] {'row_0'}, dimensions={0}, use_global_device_ids=true | all-gather | bytes 2560 | tf_op jit(solution)/shard_map/all_gather | solution.py:13
  259.1 9.0 %all-gather.23 = f32[4,1,128]{2,1,0:T(1,128)S(1)} all-gather(f32[1,1,128]{2,1,0:T(1,128)S(1)} %bitcast.41), channel_id=9, replica_groups=mesh['row_0'=4,'row_1'=4,'col'=16] {'row_1'}, dimensions={0}, use_global_device_ids=true | all-gather | bytes 2560 | tf_op jit(solution)/shard_map/all_gather | solution.py:13
  268.1 7.8 %all-gather.18 = f32[4,1,128]{2,1,0:T(1,128)S(1)} all-gather(f32[1,1,128]{2,1,0:T(1,128)S(1)} %bitcast.43), channel_id=4, replica_groups=mesh['row_0'=4,'row_1'=4,'col'=16] {'row_0'}, dimensions={0}, use_global_device_ids=true | all-gather | bytes 2560 | tf_op jit(solution)/shard_map/all_gather | solution.py:13
  275.9 8.1 %all-gather.19 = f32[4,1,128]{2,1,0:T(1,128)S(1)} all-gather(f32[1,1,128]{2,1,0:T(1,128)S(1)} %bitcast.42), channel_id=5, replica_groups=mesh['row_0'=4,'row_1'=4,'col'=16] {'row_1'}, dimensions={0}, use_global_device_ids=true | all-gather | bytes 2560 | tf_op jit(solution)/shard_map/all_gather | solution.py:13
  284.1 0.2 divide_convert_fusion.3
  284.3 0.9 pad_maximum_fusion
  (21 shorter events, 0.4 us)
Async XLA Ops:
  6.5 61.8 %all-gather.35.cloned.1.call-start = ((), (), s32[]{:S(2)}) async-start(), calls=%async_computation | async-start | bytes 8912896 | tf_op jit(solution)/shard_map/all_gather | solution.py:32
  9.4 135.8 %all-gather.37.cloned.1.call-start = ((), (), s32[]{:S(2)}) async-start(), calls=%async_computation.1 | async-start | bytes 8912896 | tf_op jit(solution)/shard_map/all_gather | solution.py:30
Sparse Core Ops, SparseCore 0:
  9.5 58.7 all-gather.34
  70.7 74.3 all-gather.36
